TPU v7x, 64 devices: a 2x2x8 block of a 4x4x8 slice. The times are simulated.
64 devices in a mesh: sys: 4 (over x, y), row: 16 (over z, core).
Axes of the slice: x: 2, y: 2, z: 8, core: 2. Of those that a mesh axis runs over, the one named last changes fastest.
The devices are a block of a 4x4x8 slice.
Arguments:
- positions: bfloat16 [131072, 128], P(('sys', 'row')), parts along dimension 0
- charges: float32 [131072], P(('sys', 'row')), parts along dimension 0
Outputs:
- output 1: float32 [131072, 128], P(('sys', 'row')), parts along dimension 0
- output 2: float32 [4], P('sys'), parts along dimension 0
There are 4 independent parts. A program takes and returns all parts, laid end to end along the dimension named above; each array names one.
All inputs are finite; a program needn't handle non-finite values.
Results may differ from a plain program's by a relative error of at most 0.001.
Values are sent between devices in bfloat16 or wider.
A program may use at most 768 MiB of HBM per device.

v0:
```python
import jax
import jax.numpy as jnp
from jax import lax
from jax.sharding import PartitionSpec as P


def pair_weight(host_x, host_q, host_sq, vis_x, vis_q, vis_sq, ell_sq):
    cross_dot = lax.dot_general(host_x, vis_x, (((1,), (1,)), ((), ())), preferred_element_type=jnp.float32)
    sq_dist = jnp.maximum(host_sq[:, None] + vis_sq[None, :] - 2.0 * cross_dot, 0.0)
    return host_q[:, None] * vis_q[None, :] * jnp.exp(-sq_dist / (2.0 * ell_sq))


def pair_forces(weight, host_x, vis_x):
    weight_bf = weight.astype(jnp.bfloat16)
    host_force = jnp.sum(weight, axis=1)[:, None] * host_x - jnp.dot(weight_bf, vis_x, preferred_element_type=jnp.float32)
    vis_force = jnp.sum(weight, axis=0)[:, None] * vis_x - lax.dot_general(weight_bf, host_x, (((0,), (0,)), ((), ())), preferred_element_type=jnp.float32)
    return host_force, vis_force


def row_sq(block_x):
    return jnp.sum(jnp.square(block_x.astype(jnp.float32)), axis=1)


def solution(mesh):
    row_count = mesh.shape["row"]
    full_steps = (row_count - 1) // 2
    has_middle = row_count % 2 == 0
    travel = row_count // 2
    forward = [(source, (source + 1) % row_count) for source in range(row_count)]
    homeward = [(source, (source - travel) % row_count) for source in range(row_count)]

    def device_body(pos_loc, chg_loc):
        rows_dev, feat_width = pos_loc.shape
        ell_sq = float(feat_width)
        half_rows = rows_dev // 2
        sq_loc = row_sq(pos_loc)
        local_ids = jnp.arange(rows_dev)
        diag_w = pair_weight(pos_loc, chg_loc, sq_loc, pos_loc, chg_loc, sq_loc, ell_sq)
        diag_w = jnp.where(local_ids[:, None] == local_ids[None, :], 0.0, diag_w)
        own_force = jnp.sum(diag_w, axis=1)[:, None] * pos_loc - jnp.dot(diag_w.astype(jnp.bfloat16), pos_loc, preferred_element_type=jnp.float32)
        own_energy = 0.5 * jnp.sum(diag_w)

        def full_step(step_idx, loop_state):
            vis_x, vis_q, vis_acc, force_acc, energy_acc = loop_state
            vis_x = lax.ppermute(vis_x, "row", forward)
            vis_q = lax.ppermute(vis_q, "row", forward)
            vis_acc = lax.ppermute(vis_acc, "row", forward)
            weight = pair_weight(pos_loc, chg_loc, sq_loc, vis_x, vis_q, row_sq(vis_x), ell_sq)
            host_force, vis_force = pair_forces(weight, pos_loc, vis_x)
            return (vis_x, vis_q, vis_acc + vis_force, force_acc + host_force, energy_acc + jnp.sum(weight))

        loop_state = (pos_loc, chg_loc, jnp.zeros((rows_dev, feat_width), jnp.float32), own_force, own_energy)
        vis_x, vis_q, vis_acc, force_acc, energy_acc = lax.fori_loop(0, full_steps, full_step, loop_state)
        if has_middle:
            vis_x = lax.ppermute(vis_x, "row", forward)
            vis_q = lax.ppermute(vis_q, "row", forward)
            vis_acc = lax.ppermute(vis_acc, "row", forward)
            vis_sq = row_sq(vis_x)
            low_half = lax.axis_index("row") < travel
            part_x = jnp.where(low_half, pos_loc[:half_rows], vis_x[half_rows:])
            part_q = jnp.where(low_half, chg_loc[:half_rows], vis_q[half_rows:])
            part_sq = jnp.where(low_half, sq_loc[:half_rows], vis_sq[half_rows:])
            other_x = jnp.where(low_half, vis_x, pos_loc)
            other_q = jnp.where(low_half, vis_q, chg_loc)
            other_sq = jnp.where(low_half, vis_sq, sq_loc)
            weight = pair_weight(part_x, part_q, part_sq, other_x, other_q, other_sq, ell_sq)
            part_force, other_force = pair_forces(weight, part_x, other_x)
            zero_half = jnp.zeros((half_rows, feat_width), jnp.float32)
            head_fill = jnp.concatenate([part_force, zero_half], axis=0)
            tail_fill = jnp.concatenate([zero_half, part_force], axis=0)
            force_acc = force_acc + jnp.where(low_half, head_fill, other_force)
            vis_acc = vis_acc + jnp.where(low_half, other_force, tail_fill)
            energy_acc = energy_acc + jnp.sum(weight)
        home_acc = lax.ppermute(vis_acc, "row", homeward)
        energy = lax.psum(energy_acc, "row")
        return (force_acc + home_acc) / ell_sq, energy.reshape(1)

    return jax.shard_map(device_body, mesh=mesh, in_specs=(P(("sys", "row"), None), P(("sys", "row"))), out_specs=(P(("sys", "row"), None), P("sys")), check_vma=False)
```

profile of v0, /device:TPU:30, one launch (start us, length us, event | category | flops | bytes accessed | tf_op | source)
XLA Modules:
  0.0 351.8 jit_solution(1394348812653871435)
XLA Ops:
  0.6 1.4 fusion.16
  2.0 1.9 copy.5
  4.0 0.7 copy.6
  4.7 13.8 %fusion.18 = (f32[]{:T(128)}, f32[2048]{0:T(1024)S(1)}, bf16[2048,2048]{0,1:T(8,128)(2,1)}) fusion(bf16[2048,128]{1,0:T(8,128)(2,1)} %param.4, f32[2048]{0:T(1024)S(1)} %fusion.16, f32[2048]{0:T(1024)} %param.5), kind=kOutput, calls=%fused_computation.37 | convolution fusion | flops 1128265728 | bytes 8937476 | tf_op jit(solution)/shard_map/dot_general | solution.py:8
  18.4 6.0 %fusion.9 = f32[2048,128]{1,0:T(8,128)S(1)} fusion(bf16[2048,128]{1,0:T(8,128)(2,1)S(1)} %copy-done.1, bf16[2048,2048]{0,1:T(8,128)(2,1)} %get-tuple-element.115, f32[2048]{0:T(1024)S(1)} %get-tuple-element.92), kind=kOutput, calls=%fused_computation.17 | convolution fusion | flops 1074528256 | bytes 9969664 | tf_op jit(solution)/shard_map/dot_general | solution.py:40
  25.0 231.8 %while.19 = (s32[]{:T(128)}, bf16[2048,128]{1,0:T(8,128)(2,1)}, f32[2048]{0:T(1024)S(1)}, f32[2048,128]{1,0:T(8,128)}, f32[2048,128]{1,0:T(8,128)S(1)}, /*index=...) while((s32[]{:T(128)}, bf16[2048,128]{1,0:T(8,128)(2,1)}, ...), condition=%wide.region_8.9_spmd.clone, body=%wide.region_3.8_spmd.clone.sunk | while | flops 3274696704 | bytes 76144928 | solution.py:53
  25.3 2.2 collective-permute-start.1
  27.5 1.0 broadcast_select_fusion.5
  28.6 10.4 %collective-permute-done.1 = f32[2048]{0:T(1024)S(1)} collective-permute-done((f32[2048]{0:T(1024)S(1)}, f32[2048]{0:T(1024)S(1)}, u32[]{:S(2)}, u32[]{:S(2)}) %collective-permute-start.1) | collective-permute-done | bytes 8224 | tf_op jit(solution)/shard_map/while/body/eval_jaxpr/ppermute | solution.py:46
  39.0 0.3 fusion.51
  39.4 10.7 %fusion.52 = (f32[]{:T(128)}, f32[2048]{0:T(1024)S(1)}, f32[2048]{0:T(1024)S(1)}, bf16[2048,2048]{1,0:T(8,128)(2,1)}) fusion(bf16[2048,128]{1,0:T(8,128)(2,1)S(1)} %get-tuple-element.223, bf16[2048,128]{1,0:T(8,128)(2,1)S(1)} %collective-permute-done, f32[2048]{0:T(1024)S(1)} %fusion.51, f32[2048]{0:T(1024)S(1)} %get-tuple-element.222, ...), kind=kOutput, calls=%fused_computation.36.clone.1 | convolution fusion | flops 1124069376 | bytes 9486340 | tf_op jit(solution)/shard_map/while/body/eval_jaxpr/dot_general | solution.py:8
  50.7 0.8 copy.17
  51.5 6.4 %subtract_add_fusion.2 = f32[2048,128]{1,0:T(8,128)S(1)} fusion(f32[2048,128]{1,0:T(8,128)S(1)} %get-tuple-element.208, bf16[2048,128]{1,0:T(8,128)(2,1)S(1)} %get-tuple-element.223, f32[2048]{0:T(1024)S(1)} %get-tuple-element.191, bf16[2048,128]{1,0:T(8,128)(2,1)S(1)} %collective-permute-done, bf16[2048,2048]{1,0:T(8,128)(2,1)} %get-tuple-element.190), kind=kOutput, calls=%fused_computation.10.clone.1 | convolution fusion | flops 1074790400 | bytes 11542528 | tf_op jit(solution)/shard_map/while/body/eval_jaxpr/dot_general | solution.py:15
  58.0 3.7 %fusion.53 = f32[2048,128]{1,0:T(8,128)} fusion(f32[2048,128]{1,0:T(8,128)S(1)} %collective-permute-done.2, bf16[2048,128]{1,0:T(8,128)(2,1)S(1)} %collective-permute-done, f32[2048]{0:T(1024)S(1)} %get-tuple-element.189, bf16[2048,128]{1,0:T(8,128)(2,1)S(1)} %get-tuple-element.223, bf16[2048,2048]{1,0:T(8,128)(2,1)S(1)} %copy-done), kind=kOutput, calls=%fused_computation.9.clone.1 | convolution fusion | flops 1074790400 | bytes 11542528 | tf_op jit(solution)/shard_map/while/body/eval_jaxpr/dot_general | solution.py:16
  61.7 2.3 broadcast_select_fusion.5
  63.9 7.6 %collective-permute-done.1 = f32[2048]{0:T(1024)S(1)} collective-permute-done((f32[2048]{0:T(1024)S(1)}, f32[2048]{0:T(1024)S(1)}, u32[]{:S(2)}, u32[]{:S(2)}) %collective-permute-start.1) | collective-permute-done | bytes 8224 | tf_op jit(solution)/shard_map/while/body/eval_jaxpr/ppermute | solution.py:46
  71.6 0.3 fusion.51
  71.9 10.7 %fusion.52 = (f32[]{:T(128)}, f32[2048]{0:T(1024)S(1)}, f32[2048]{0:T(1024)S(1)}, bf16[2048,2048]{1,0:T(8,128)(2,1)}) fusion(bf16[2048,128]{1,0:T(8,128)(2,1)S(1)} %get-tuple-element.223, bf16[2048,128]{1,0:T(8,128)(2,1)S(1)} %collective-permute-done, f32[2048]{0:T(1024)S(1)} %fusion.51, f32[2048]{0:T(1024)S(1)} %get-tuple-element.222, ...), kind=kOutput, calls=%fused_computation.36.clone.1 | convolution fusion | flops 1124069376 | bytes 9486340 | tf_op jit(solution)/shard_map/while/body/eval_jaxpr/dot_general | solution.py:8
  83.2 0.8 copy.17
  84.1 6.4 %subtract_add_fusion.2 = f32[2048,128]{1,0:T(8,128)S(1)} fusion(f32[2048,128]{1,0:T(8,128)S(1)} %get-tuple-element.208, bf16[2048,128]{1,0:T(8,128)(2,1)S(1)} %get-tuple-element.223, f32[2048]{0:T(1024)S(1)} %get-tuple-element.191, bf16[2048,128]{1,0:T(8,128)(2,1)S(1)} %collective-permute-done, bf16[2048,2048]{1,0:T(8,128)(2,1)} %get-tuple-element.190), kind=kOutput, calls=%fused_computation.10.clone.1 | convolution fusion | flops 1074790400 | bytes 11542528 | tf_op jit(solution)/shard_map/while/body/eval_jaxpr/dot_general | solution.py:15
  90.5 3.7 %fusion.53 = f32[2048,128]{1,0:T(8,128)} fusion(f32[2048,128]{1,0:T(8,128)S(1)} %collective-permute-done.2, bf16[2048,128]{1,0:T(8,128)(2,1)S(1)} %collective-permute-done, f32[2048]{0:T(1024)S(1)} %get-tuple-element.189, bf16[2048,128]{1,0:T(8,128)(2,1)S(1)} %get-tuple-element.223, bf16[2048,2048]{1,0:T(8,128)(2,1)S(1)} %copy-done), kind=kOutput, calls=%fused_computation.9.clone.1 | convolution fusion | flops 1074790400 | bytes 11542528 | tf_op jit(solution)/shard_map/while/body/eval_jaxpr/dot_general | solution.py:16
  94.2 2.3 broadcast_select_fusion.5
  96.5 7.6 %collective-permute-done.1 = f32[2048]{0:T(1024)S(1)} collective-permute-done((f32[2048]{0:T(1024)S(1)}, f32[2048]{0:T(1024)S(1)}, u32[]{:S(2)}, u32[]{:S(2)}) %collective-permute-start.1) | collective-permute-done | bytes 8224 | tf_op jit(solution)/shard_map/while/body/eval_jaxpr/ppermute | solution.py:46
  104.1 0.3 fusion.51
  104.5 10.7 %fusion.52 = (f32[]{:T(128)}, f32[2048]{0:T(1024)S(1)}, f32[2048]{0:T(1024)S(1)}, bf16[2048,2048]{1,0:T(8,128)(2,1)}) fusion(bf16[2048,128]{1,0:T(8,128)(2,1)S(1)} %get-tuple-element.223, bf16[2048,128]{1,0:T(8,128)(2,1)S(1)} %collective-permute-done, f32[2048]{0:T(1024)S(1)} %fusion.51, f32[2048]{0:T(1024)S(1)} %get-tuple-element.222, ...), kind=kOutput, calls=%fused_computation.36.clone.1 | convolution fusion | flops 1124069376 | bytes 9486340 | tf_op jit(solution)/shard_map/while/body/eval_jaxpr/dot_general | solution.py:8
  115.7 0.8 copy.17
  116.6 6.4 %subtract_add_fusion.2 = f32[2048,128]{1,0:T(8,128)S(1)} fusion(f32[2048,128]{1,0:T(8,128)S(1)} %get-tuple-element.208, bf16[2048,128]{1,0:T(8,128)(2,1)S(1)} %get-tuple-element.223, f32[2048]{0:T(1024)S(1)} %get-tuple-element.191, bf16[2048,128]{1,0:T(8,128)(2,1)S(1)} %collective-permute-done, bf16[2048,2048]{1,0:T(8,128)(2,1)} %get-tuple-element.190), kind=kOutput, calls=%fused_computation.10.clone.1 | convolution fusion | flops 1074790400 | bytes 11542528 | tf_op jit(solution)/shard_map/while/body/eval_jaxpr/dot_general | solution.py:15
  123.0 3.7 %fusion.53 = f32[2048,128]{1,0:T(8,128)} fusion(f32[2048,128]{1,0:T(8,128)S(1)} %collective-permute-done.2, bf16[2048,128]{1,0:T(8,128)(2,1)S(1)} %collective-permute-done, f32[2048]{0:T(1024)S(1)} %get-tuple-element.189, bf16[2048,128]{1,0:T(8,128)(2,1)S(1)} %get-tuple-element.223, bf16[2048,2048]{1,0:T(8,128)(2,1)S(1)} %copy-done), kind=kOutput, calls=%fused_computation.9.clone.1 | convolution fusion | flops 1074790400 | bytes 11542528 | tf_op jit(solution)/shard_map/while/body/eval_jaxpr/dot_general | solution.py:16
  126.7 2.3 broadcast_select_fusion.5
  129.0 7.6 %collective-permute-done.1 = f32[2048]{0:T(1024)S(1)} collective-permute-done((f32[2048]{0:T(1024)S(1)}, f32[2048]{0:T(1024)S(1)}, u32[]{:S(2)}, u32[]{:S(2)}) %collective-permute-start.1) | collective-permute-done | bytes 8224 | tf_op jit(solution)/shard_map/while/body/eval_jaxpr/ppermute | solution.py:46
  136.6 0.3 fusion.51
  137.0 10.7 %fusion.52 = (f32[]{:T(128)}, f32[2048]{0:T(1024)S(1)}, f32[2048]{0:T(1024)S(1)}, bf16[2048,2048]{1,0:T(8,128)(2,1)}) fusion(bf16[2048,128]{1,0:T(8,128)(2,1)S(1)} %get-tuple-element.223, bf16[2048,128]{1,0:T(8,128)(2,1)S(1)} %collective-permute-done, f32[2048]{0:T(1024)S(1)} %fusion.51, f32[2048]{0:T(1024)S(1)} %get-tuple-element.222, ...), kind=kOutput, calls=%fused_computation.36.clone.1 | convolution fusion | flops 1124069376 | bytes 9486340 | tf_op jit(solution)/shard_map/while/body/eval_jaxpr/dot_general | solution.py:8
  148.3 0.8 copy.17
  149.1 6.4 %subtract_add_fusion.2 = f32[2048,128]{1,0:T(8,128)S(1)} fusion(f32[2048,128]{1,0:T(8,128)S(1)} %get-tuple-element.208, bf16[2048,128]{1,0:T(8,128)(2,1)S(1)} %get-tuple-element.223, f32[2048]{0:T(1024)S(1)} %get-tuple-element.191, bf16[2048,128]{1,0:T(8,128)(2,1)S(1)} %collective-permute-done, bf16[2048,2048]{1,0:T(8,128)(2,1)} %get-tuple-element.190), kind=kOutput, calls=%fused_computation.10.clone.1 | convolution fusion | flops 1074790400 | bytes 11542528 | tf_op jit(solution)/shard_map/while/body/eval_jaxpr/dot_general | solution.py:15
  155.5 3.7 %fusion.53 = f32[2048,128]{1,0:T(8,128)} fusion(f32[2048,128]{1,0:T(8,128)S(1)} %collective-permute-done.2, bf16[2048,128]{1,0:T(8,128)(2,1)S(1)} %collective-permute-done, f32[2048]{0:T(1024)S(1)} %get-tuple-element.189, bf16[2048,128]{1,0:T(8,128)(2,1)S(1)} %get-tuple-element.223, bf16[2048,2048]{1,0:T(8,128)(2,1)S(1)} %copy-done), kind=kOutput, calls=%fused_computation.9.clone.1 | convolution fusion | flops 1074790400 | bytes 11542528 | tf_op jit(solution)/shard_map/while/body/eval_jaxpr/dot_general | solution.py:16
  159.3 2.3 broadcast_select_fusion.5
  161.5 7.6 %collective-permute-done.1 = f32[2048]{0:T(1024)S(1)} collective-permute-done((f32[2048]{0:T(1024)S(1)}, f32[2048]{0:T(1024)S(1)}, u32[]{:S(2)}, u32[]{:S(2)}) %collective-permute-start.1) | collective-permute-done | bytes 8224 | tf_op jit(solution)/shard_map/while/body/eval_jaxpr/ppermute | solution.py:46
  169.2 0.3 fusion.51
  169.5 10.7 %fusion.52 = (f32[]{:T(128)}, f32[2048]{0:T(1024)S(1)}, f32[2048]{0:T(1024)S(1)}, bf16[2048,2048]{1,0:T(8,128)(2,1)}) fusion(bf16[2048,128]{1,0:T(8,128)(2,1)S(1)} %get-tuple-element.223, bf16[2048,128]{1,0:T(8,128)(2,1)S(1)} %collective-permute-done, f32[2048]{0:T(1024)S(1)} %fusion.51, f32[2048]{0:T(1024)S(1)} %get-tuple-element.222, ...), kind=kOutput, calls=%fused_computation.36.clone.1 | convolution fusion | flops 1124069376 | bytes 9486340 | tf_op jit(solution)/shard_map/while/body/eval_jaxpr/dot_general | solution.py:8
  180.8 0.8 copy.17
  181.6 6.4 %subtract_add_fusion.2 = f32[2048,128]{1,0:T(8,128)S(1)} fusion(f32[2048,128]{1,0:T(8,128)S(1)} %get-tuple-element.208, bf16[2048,128]{1,0:T(8,128)(2,1)S(1)} %get-tuple-element.223, f32[2048]{0:T(1024)S(1)} %get-tuple-element.191, bf16[2048,128]{1,0:T(8,128)(2,1)S(1)} %collective-permute-done, bf16[2048,2048]{1,0:T(8,128)(2,1)} %get-tuple-element.190), kind=kOutput, calls=%fused_computation.10.clone.1 | convolution fusion | flops 1074790400 | bytes 11542528 | tf_op jit(solution)/shard_map/while/body/eval_jaxpr/dot_general | solution.py:15
  188.1 3.7 %fusion.53 = f32[2048,128]{1,0:T(8,128)} fusion(f32[2048,128]{1,0:T(8,128)S(1)} %collective-permute-done.2, bf16[2048,128]{1,0:T(8,128)(2,1)S(1)} %collective-permute-done, f32[2048]{0:T(1024)S(1)} %get-tuple-element.189, bf16[2048,128]{1,0:T(8,128)(2,1)S(1)} %get-tuple-element.223, bf16[2048,2048]{1,0:T(8,128)(2,1)S(1)} %copy-done), kind=kOutput, calls=%fused_computation.9.clone.1 | convolution fusion | flops 1074790400 | bytes 11542528 | tf_op jit(solution)/shard_map/while/body/eval_jaxpr/dot_general | solution.py:16
  191.8 2.3 broadcast_select_fusion.5
  194.1 7.6 %collective-permute-done.1 = f32[2048]{0:T(1024)S(1)} collective-permute-done((f32[2048]{0:T(1024)S(1)}, f32[2048]{0:T(1024)S(1)}, u32[]{:S(2)}, u32[]{:S(2)}) %collective-permute-start.1) | collective-permute-done | bytes 8224 | tf_op jit(solution)/shard_map/while/body/eval_jaxpr/ppermute | solution.py:46
  201.7 0.3 fusion.51
  202.1 10.7 %fusion.52 = (f32[]{:T(128)}, f32[2048]{0:T(1024)S(1)}, f32[2048]{0:T(1024)S(1)}, bf16[2048,2048]{1,0:T(8,128)(2,1)}) fusion(bf16[2048,128]{1,0:T(8,128)(2,1)S(1)} %get-tuple-element.223, bf16[2048,128]{1,0:T(8,128)(2,1)S(1)} %collective-permute-done, f32[2048]{0:T(1024)S(1)} %fusion.51, f32[2048]{0:T(1024)S(1)} %get-tuple-element.222, ...), kind=kOutput, calls=%fused_computation.36.clone.1 | convolution fusion | flops 1124069376 | bytes 9486340 | tf_op jit(solution)/shard_map/while/body/eval_jaxpr/dot_general | solution.py:8
  213.3 0.8 copy.17
  214.2 6.4 %subtract_add_fusion.2 = f32[2048,128]{1,0:T(8,128)S(1)} fusion(f32[2048,128]{1,0:T(8,128)S(1)} %get-tuple-element.208, bf16[2048,128]{1,0:T(8,128)(2,1)S(1)} %get-tuple-element.223, f32[2048]{0:T(1024)S(1)} %get-tuple-element.191, bf16[2048,128]{1,0:T(8,128)(2,1)S(1)} %collective-permute-done, bf16[2048,2048]{1,0:T(8,128)(2,1)} %get-tuple-element.190), kind=kOutput, calls=%fused_computation.10.clone.1 | convolution fusion | flops 1074790400 | bytes 11542528 | tf_op jit(solution)/shard_map/while/body/eval_jaxpr/dot_general | solution.py:15
  220.6 3.7 %fusion.53 = f32[2048,128]{1,0:T(8,128)} fusion(f32[2048,128]{1,0:T(8,128)S(1)} %collective-permute-done.2, bf16[2048,128]{1,0:T(8,128)(2,1)S(1)} %collective-permute-done, f32[2048]{0:T(1024)S(1)} %get-tuple-element.189, bf16[2048,128]{1,0:T(8,128)(2,1)S(1)} %get-tuple-element.223, bf16[2048,2048]{1,0:T(8,128)(2,1)S(1)} %copy-done), kind=kOutput, calls=%fused_computation.9.clone.1 | convolution fusion | flops 1074790400 | bytes 11542528 | tf_op jit(solution)/shard_map/while/body/eval_jaxpr/dot_general | solution.py:16
  224.3 2.3 broadcast_select_fusion.5
  226.6 7.6 %collective-permute-done.1 = f32[2048]{0:T(1024)S(1)} collective-permute-done((f32[2048]{0:T(1024)S(1)}, f32[2048]{0:T(1024)S(1)}, u32[]{:S(2)}, u32[]{:S(2)}) %collective-permute-start.1) | collective-permute-done | bytes 8224 | tf_op jit(solution)/shard_map/while/body/eval_jaxpr/ppermute | solution.py:46
  234.6 10.7 %fusion.52 = (f32[]{:T(128)}, f32[2048]{0:T(1024)S(1)}, f32[2048]{0:T(1024)S(1)}, bf16[2048,2048]{1,0:T(8,128)(2,1)}) fusion(bf16[2048,128]{1,0:T(8,128)(2,1)S(1)} %get-tuple-element.223, bf16[2048,128]{1,0:T(8,128)(2,1)S(1)} %collective-permute-done, f32[2048]{0:T(1024)S(1)} %fusion.51, f32[2048]{0:T(1024)S(1)} %get-tuple-element.222, ...), kind=kOutput, calls=%fused_computation.36.clone.1 | convolution fusion | flops 1124069376 | bytes 9486340 | tf_op jit(solution)/shard_map/while/body/eval_jaxpr/dot_general | solution.py:8
  245.9 0.8 copy.17
  246.7 6.4 %subtract_add_fusion.2 = f32[2048,128]{1,0:T(8,128)S(1)} fusion(f32[2048,128]{1,0:T(8,128)S(1)} %get-tuple-element.208, bf16[2048,128]{1,0:T(8,128)(2,1)S(1)} %get-tuple-element.223, f32[2048]{0:T(1024)S(1)} %get-tuple-element.191, bf16[2048,128]{1,0:T(8,128)(2,1)S(1)} %collective-permute-done, bf16[2048,2048]{1,0:T(8,128)(2,1)} %get-tuple-element.190), kind=kOutput, calls=%fused_computation.10.clone.1 | convolution fusion | flops 1074790400 | bytes 11542528 | tf_op jit(solution)/shard_map/while/body/eval_jaxpr/dot_general | solution.py:15
  253.1 3.7 %fusion.53 = f32[2048,128]{1,0:T(8,128)} fusion(f32[2048,128]{1,0:T(8,128)S(1)} %collective-permute-done.2, bf16[2048,128]{1,0:T(8,128)(2,1)S(1)} %collective-permute-done, f32[2048]{0:T(1024)S(1)} %get-tuple-element.189, bf16[2048,128]{1,0:T(8,128)(2,1)S(1)} %get-tuple-element.223, bf16[2048,2048]{1,0:T(8,128)(2,1)S(1)} %copy-done), kind=kOutput, calls=%fused_computation.9.clone.1 | convolution fusion | flops 1074790400 | bytes 11542528 | tf_op jit(solution)/shard_map/while/body/eval_jaxpr/dot_general | solution.py:16
  256.9 9.9 %collective-permute-done.3 = f32[2048]{0:T(1024)S(1)} collective-permute-done((f32[2048]{0:T(1024)S(1)}, f32[2048]{0:T(1024)S(1)}, u32[]{:S(2)}, u32[]{:S(2)}) %collective-permute-start.3) | collective-permute-done | bytes 8224 | tf_op jit(solution)/shard_map/ppermute | solution.py:56
  266.8 0.3 multiply_reduce_fusion
  267.3 5.2 %fusion.19 = (f32[]{:T(128)}, f32[2048]{0:T(1024)S(1)}, f32[1024]{0:T(1024)S(1)}, bf16[1024,2048]{1,0:T(8,128)(2,1)S(1)}) fusion(bf16[1024,128]{1,0:T(8,128)(2,1)S(1)} %slice_select_fusion, bf16[2048,128]{1,0:T(8,128)(2,1)S(1)} %broadcast_select_fusion.1, f32[2048]{0:T(1024)S(1)} %broadcast_select_fusion.2, f32[1024]{0:T(1024)S(1)} %slice_select_fusion.1, ...), kind=kOutput, calls=%fused_computation.38 | convolution fusion | flops 562033664 | bytes 5017604 | tf_op jit(solution)/shard_map/dot_general | solution.py:8
  272.5 1.2 multiply_subtract_fusion.1
  273.7 37.5 %collective-permute-done.5 = f32[2048,128]{1,0:T(8,128)} collective-permute-done((f32[2048,128]{1,0:T(8,128)}, f32[2048,128]{1,0:T(8,128)}, u32[]{:S(2)}, u32[]{:S(2)}) %collective-permute-start.5) | collective-permute-done | bytes 1048608 | tf_op jit(solution)/shard_map/ppermute | solution.py:57
  311.2 3.7 %select_add_fusion = (f32[2048,128]{1,0:T(8,128)}, f32[2048,128]{1,0:T(8,128)S(1)}) fusion(f32[2048,128]{1,0:T(8,128)} %collective-permute-done.5, f32[1024,128]{1,0:T(8,128)S(1)} %multiply_subtract_fusion.1, bf16[2048,128]{1,0:T(8,128)(2,1)S(1)} %broadcast_select_fusion.1, f32[2048]{0:T(1024)S(1)} %get-tuple-element.94, pred[]{:T(512)S(6)} %lt.6, ...), kind=kOutput, calls=%fused_computation.26 | convolution fusion | flops 538181632 | bytes 8658945 | tf_op jit(solution)/shard_map/dot_general | solution.py:16
  315.0 2.1 collective-permute-start.6
  317.7 31.5 %psum.7 = f32[1]{0:T(128)} all-reduce(f32[1]{0:T(128)} %bitcast), channel_id=1, replica_groups=mesh['sys'=4,'row'=16] {'row'}, use_global_device_ids=true, to_apply=%region_13.14 | all-reduce | flops 1 | bytes 8 | tf_op jit(solution)/shard_map/psum | solution.py:75
  349.2 2.6 add_multiply_fusion
  (72 shorter events, 0.7 us)
Async XLA Ops:
  4.7 13.8 %copy-start.1 = (bf16[2048,128]{1,0:T(8,128)(2,1)S(1)}, bf16[2048,128]{1,0:T(8,128)(2,1)}, u32[]{:S(2)}) copy-start(bf16[2048,128]{1,0:T(8,128)(2,1)} %param.4) | copy-start | bytes 1572868
  18.4 6.6 %copy-start.2 = (f32[2048]{0:T(1024)S(1)}, f32[2048]{0:T(1024)}, u32[]{:S(2)}) copy-start(f32[2048]{0:T(1024)} %param.5) | copy-start | bytes 24580
  25.2 13.8 %collective-permute-start = (bf16[2048,128]{1,0:T(8,128)(2,1)}, bf16[2048,128]{1,0:T(8,128)(2,1)S(1)}, u32[]{:S(2)}, u32[]{:S(2)}) collective-permute-start(bf16[2048,128]{1,0:T(8,128)(2,1)} %get-tuple-element.205), channel_id=1, source_target_pairs={{0,1},{1,2},{2,3},{3,4},{4,5},{5,6},{6,7},{7,8},{8,9},{9,10},{10,1... | collective-permute-start | bytes 1572872 | tf_op jit(solution)/shard_map/while/body/eval_jaxpr/ppermute | solution.py:45
  25.3 13.7 %collective-permute-start.1 = (f32[2048]{0:T(1024)S(1)}, f32[2048]{0:T(1024)S(1)}, u32[]{:S(2)}, u32[]{:S(2)}) collective-permute-start(f32[2048]{0:T(1024)S(1)} %get-tuple-element.206), channel_id=1, source_target_pairs={{0,1},{1,2},{2,3},{3,4},{4,5},{5,6},{6,7},{7,8},{8,9},{9,10},{10,1... | collective-permute-start | bytes 24584 | tf_op jit(solution)/shard_map/while/body/eval_jaxpr/ppermute | solution.py:46
  28.6 29.4 %collective-permute-start.2 = (f32[2048,128]{1,0:T(8,128)}, f32[2048,128]{1,0:T(8,128)S(1)}, u32[]{:S(2)}, u32[]{:S(2)}) collective-permute-start(f32[2048,128]{1,0:T(8,128)} %broadcast_select_fusion.5), channel_id=1, source_target_pairs={{0,1},{1,2},{2,3},{3,4},{4,5},{5,6},{6,7},{7,8},{8,9},{9,10},{10,1... | collective-permute-start | bytes 3145736 | tf_op jit(solution)/shard_map/while/body/eval_jaxpr/ppermute | solution.py:47
  50.7 7.3 %copy-start = (bf16[2048,2048]{1,0:T(8,128)(2,1)S(1)}, bf16[2048,2048]{1,0:T(8,128)(2,1)}, u32[]{:S(2)}) copy-start(bf16[2048,2048]{1,0:T(8,128)(2,1)} %get-tuple-element.190) | copy-start | bytes 25165828 | tf_op jit(solution)/shard_map/while
  61.7 9.9 %collective-permute-start = (bf16[2048,128]{1,0:T(8,128)(2,1)}, bf16[2048,128]{1,0:T(8,128)(2,1)S(1)}, u32[]{:S(2)}, u32[]{:S(2)}) collective-permute-start(bf16[2048,128]{1,0:T(8,128)(2,1)} %get-tuple-element.205), channel_id=1, source_target_pairs={{0,1},{1,2},{2,3},{3,4},{4,5},{5,6},{6,7},{7,8},{8,9},{9,10},{10,1... | collective-permute-start | bytes 1572872 | tf_op jit(solution)/shard_map/while/body/eval_jaxpr/ppermute | solution.py:45
  61.7 9.9 %collective-permute-start.1 = (f32[2048]{0:T(1024)S(1)}, f32[2048]{0:T(1024)S(1)}, u32[]{:S(2)}, u32[]{:S(2)}) collective-permute-start(f32[2048]{0:T(1024)S(1)} %get-tuple-element.206), channel_id=1, source_target_pairs={{0,1},{1,2},{2,3},{3,4},{4,5},{5,6},{6,7},{7,8},{8,9},{9,10},{10,1... | collective-permute-start | bytes 24584 | tf_op jit(solution)/shard_map/while/body/eval_jaxpr/ppermute | solution.py:46
  63.9 26.5 %collective-permute-start.2 = (f32[2048,128]{1,0:T(8,128)}, f32[2048,128]{1,0:T(8,128)S(1)}, u32[]{:S(2)}, u32[]{:S(2)}) collective-permute-start(f32[2048,128]{1,0:T(8,128)} %broadcast_select_fusion.5), channel_id=1, source_target_pairs={{0,1},{1,2},{2,3},{3,4},{4,5},{5,6},{6,7},{7,8},{8,9},{9,10},{10,1... | collective-permute-start | bytes 3145736 | tf_op jit(solution)/shard_map/while/body/eval_jaxpr/ppermute | solution.py:47
  83.2 7.3 %copy-start = (bf16[2048,2048]{1,0:T(8,128)(2,1)S(1)}, bf16[2048,2048]{1,0:T(8,128)(2,1)}, u32[]{:S(2)}) copy-start(bf16[2048,2048]{1,0:T(8,128)(2,1)} %get-tuple-element.190) | copy-start | bytes 25165828 | tf_op jit(solution)/shard_map/while
  94.2 9.9 %collective-permute-start = (bf16[2048,128]{1,0:T(8,128)(2,1)}, bf16[2048,128]{1,0:T(8,128)(2,1)S(1)}, u32[]{:S(2)}, u32[]{:S(2)}) collective-permute-start(bf16[2048,128]{1,0:T(8,128)(2,1)} %get-tuple-element.205), channel_id=1, source_target_pairs={{0,1},{1,2},{2,3},{3,4},{4,5},{5,6},{6,7},{7,8},{8,9},{9,10},{10,1... | collective-permute-start | bytes 1572872 | tf_op jit(solution)/shard_map/while/body/eval_jaxpr/ppermute | solution.py:45
  94.2 9.9 %collective-permute-start.1 = (f32[2048]{0:T(1024)S(1)}, f32[2048]{0:T(1024)S(1)}, u32[]{:S(2)}, u32[]{:S(2)}) collective-permute-start(f32[2048]{0:T(1024)S(1)} %get-tuple-element.206), channel_id=1, source_target_pairs={{0,1},{1,2},{2,3},{3,4},{4,5},{5,6},{6,7},{7,8},{8,9},{9,10},{10,1... | collective-permute-start | bytes 24584 | tf_op jit(solution)/shard_map/while/body/eval_jaxpr/ppermute | solution.py:46
  96.5 26.5 %collective-permute-start.2 = (f32[2048,128]{1,0:T(8,128)}, f32[2048,128]{1,0:T(8,128)S(1)}, u32[]{:S(2)}, u32[]{:S(2)}) collective-permute-start(f32[2048,128]{1,0:T(8,128)} %broadcast_select_fusion.5), channel_id=1, source_target_pairs={{0,1},{1,2},{2,3},{3,4},{4,5},{5,6},{6,7},{7,8},{8,9},{9,10},{10,1... | collective-permute-start | bytes 3145736 | tf_op jit(solution)/shard_map/while/body/eval_jaxpr/ppermute | solution.py:47
  115.7 7.3 %copy-start = (bf16[2048,2048]{1,0:T(8,128)(2,1)S(1)}, bf16[2048,2048]{1,0:T(8,128)(2,1)}, u32[]{:S(2)}) copy-start(bf16[2048,2048]{1,0:T(8,128)(2,1)} %get-tuple-element.190) | copy-start | bytes 25165828 | tf_op jit(solution)/shard_map/while
  126.7 9.9 %collective-permute-start = (bf16[2048,128]{1,0:T(8,128)(2,1)}, bf16[2048,128]{1,0:T(8,128)(2,1)S(1)}, u32[]{:S(2)}, u32[]{:S(2)}) collective-permute-start(bf16[2048,128]{1,0:T(8,128)(2,1)} %get-tuple-element.205), channel_id=1, source_target_pairs={{0,1},{1,2},{2,3},{3,4},{4,5},{5,6},{6,7},{7,8},{8,9},{9,10},{10,1... | collective-permute-start | bytes 1572872 | tf_op jit(solution)/shard_map/while/body/eval_jaxpr/ppermute | solution.py:45
  126.7 9.9 %collective-permute-start.1 = (f32[2048]{0:T(1024)S(1)}, f32[2048]{0:T(1024)S(1)}, u32[]{:S(2)}, u32[]{:S(2)}) collective-permute-start(f32[2048]{0:T(1024)S(1)} %get-tuple-element.206), channel_id=1, source_target_pairs={{0,1},{1,2},{2,3},{3,4},{4,5},{5,6},{6,7},{7,8},{8,9},{9,10},{10,1... | collective-permute-start | bytes 24584 | tf_op jit(solution)/shard_map/while/body/eval_jaxpr/ppermute | solution.py:46
  129.0 26.5 %collective-permute-start.2 = (f32[2048,128]{1,0:T(8,128)}, f32[2048,128]{1,0:T(8,128)S(1)}, u32[]{:S(2)}, u32[]{:S(2)}) collective-permute-start(f32[2048,128]{1,0:T(8,128)} %broadcast_select_fusion.5), channel_id=1, source_target_pairs={{0,1},{1,2},{2,3},{3,4},{4,5},{5,6},{6,7},{7,8},{8,9},{9,10},{10,1... | collective-permute-start | bytes 3145736 | tf_op jit(solution)/shard_map/while/body/eval_jaxpr/ppermute | solution.py:47
  148.3 7.3 %copy-start = (bf16[2048,2048]{1,0:T(8,128)(2,1)S(1)}, bf16[2048,2048]{1,0:T(8,128)(2,1)}, u32[]{:S(2)}) copy-start(bf16[2048,2048]{1,0:T(8,128)(2,1)} %get-tuple-element.190) | copy-start | bytes 25165828 | tf_op jit(solution)/shard_map/while
  159.3 9.9 %collective-permute-start = (bf16[2048,128]{1,0:T(8,128)(2,1)}, bf16[2048,128]{1,0:T(8,128)(2,1)S(1)}, u32[]{:S(2)}, u32[]{:S(2)}) collective-permute-start(bf16[2048,128]{1,0:T(8,128)(2,1)} %get-tuple-element.205), channel_id=1, source_target_pairs={{0,1},{1,2},{2,3},{3,4},{4,5},{5,6},{6,7},{7,8},{8,9},{9,10},{10,1... | collective-permute-start | bytes 1572872 | tf_op jit(solution)/shard_map/while/body/eval_jaxpr/ppermute | solution.py:45
  159.3 9.9 %collective-permute-start.1 = (f32[2048]{0:T(1024)S(1)}, f32[2048]{0:T(1024)S(1)}, u32[]{:S(2)}, u32[]{:S(2)}) collective-permute-start(f32[2048]{0:T(1024)S(1)} %get-tuple-element.206), channel_id=1, source_target_pairs={{0,1},{1,2},{2,3},{3,4},{4,5},{5,6},{6,7},{7,8},{8,9},{9,10},{10,1... | collective-permute-start | bytes 24584 | tf_op jit(solution)/shard_map/while/body/eval_jaxpr/ppermute | solution.py:46
  161.5 26.5 %collective-permute-start.2 = (f32[2048,128]{1,0:T(8,128)}, f32[2048,128]{1,0:T(8,128)S(1)}, u32[]{:S(2)}, u32[]{:S(2)}) collective-permute-start(f32[2048,128]{1,0:T(8,128)} %broadcast_select_fusion.5), channel_id=1, source_target_pairs={{0,1},{1,2},{2,3},{3,4},{4,5},{5,6},{6,7},{7,8},{8,9},{9,10},{10,1... | collective-permute-start | bytes 3145736 | tf_op jit(solution)/shard_map/while/body/eval_jaxpr/ppermute | solution.py:47
  180.8 7.3 %copy-start = (bf16[2048,2048]{1,0:T(8,128)(2,1)S(1)}, bf16[2048,2048]{1,0:T(8,128)(2,1)}, u32[]{:S(2)}) copy-start(bf16[2048,2048]{1,0:T(8,128)(2,1)} %get-tuple-element.190) | copy-start | bytes 25165828 | tf_op jit(solution)/shard_map/while
  191.8 9.9 %collective-permute-start = (bf16[2048,128]{1,0:T(8,128)(2,1)}, bf16[2048,128]{1,0:T(8,128)(2,1)S(1)}, u32[]{:S(2)}, u32[]{:S(2)}) collective-permute-start(bf16[2048,128]{1,0:T(8,128)(2,1)} %get-tuple-element.205), channel_id=1, source_target_pairs={{0,1},{1,2},{2,3},{3,4},{4,5},{5,6},{6,7},{7,8},{8,9},{9,10},{10,1... | collective-permute-start | bytes 1572872 | tf_op jit(solution)/shard_map/while/body/eval_jaxpr/ppermute | solution.py:45
  191.8 9.9 %collective-permute-start.1 = (f32[2048]{0:T(1024)S(1)}, f32[2048]{0:T(1024)S(1)}, u32[]{:S(2)}, u32[]{:S(2)}) collective-permute-start(f32[2048]{0:T(1024)S(1)} %get-tuple-element.206), channel_id=1, source_target_pairs={{0,1},{1,2},{2,3},{3,4},{4,5},{5,6},{6,7},{7,8},{8,9},{9,10},{10,1... | collective-permute-start | bytes 24584 | tf_op jit(solution)/shard_map/while/body/eval_jaxpr/ppermute | solution.py:46
  194.1 26.5 %collective-permute-start.2 = (f32[2048,128]{1,0:T(8,128)}, f32[2048,128]{1,0:T(8,128)S(1)}, u32[]{:S(2)}, u32[]{:S(2)}) collective-permute-start(f32[2048,128]{1,0:T(8,128)} %broadcast_select_fusion.5), channel_id=1, source_target_pairs={{0,1},{1,2},{2,3},{3,4},{4,5},{5,6},{6,7},{7,8},{8,9},{9,10},{10,1... | collective-permute-start | bytes 3145736 | tf_op jit(solution)/shard_map/while/body/eval_jaxpr/ppermute | solution.py:47
  213.3 7.3 %copy-start = (bf16[2048,2048]{1,0:T(8,128)(2,1)S(1)}, bf16[2048,2048]{1,0:T(8,128)(2,1)}, u32[]{:S(2)}) copy-start(bf16[2048,2048]{1,0:T(8,128)(2,1)} %get-tuple-element.190) | copy-start | bytes 25165828 | tf_op jit(solution)/shard_map/while
  224.3 9.9 %collective-permute-start = (bf16[2048,128]{1,0:T(8,128)(2,1)}, bf16[2048,128]{1,0:T(8,128)(2,1)S(1)}, u32[]{:S(2)}, u32[]{:S(2)}) collective-permute-start(bf16[2048,128]{1,0:T(8,128)(2,1)} %get-tuple-element.205), channel_id=1, source_target_pairs={{0,1},{1,2},{2,3},{3,4},{4,5},{5,6},{6,7},{7,8},{8,9},{9,10},{10,1... | collective-permute-start | bytes 1572872 | tf_op jit(solution)/shard_map/while/body/eval_jaxpr/ppermute | solution.py:45
  224.3 9.9 %collective-permute-start.1 = (f32[2048]{0:T(1024)S(1)}, f32[2048]{0:T(1024)S(1)}, u32[]{:S(2)}, u32[]{:S(2)}) collective-permute-start(f32[2048]{0:T(1024)S(1)} %get-tuple-element.206), channel_id=1, source_target_pairs={{0,1},{1,2},{2,3},{3,4},{4,5},{5,6},{6,7},{7,8},{8,9},{9,10},{10,1... | collective-permute-start | bytes 24584 | tf_op jit(solution)/shard_map/while/body/eval_jaxpr/ppermute | solution.py:46
  226.6 26.5 %collective-permute-start.2 = (f32[2048,128]{1,0:T(8,128)}, f32[2048,128]{1,0:T(8,128)S(1)}, u32[]{:S(2)}, u32[]{:S(2)}) collective-permute-start(f32[2048,128]{1,0:T(8,128)} %broadcast_select_fusion.5), channel_id=1, source_target_pairs={{0,1},{1,2},{2,3},{3,4},{4,5},{5,6},{6,7},{7,8},{8,9},{9,10},{10,1... | collective-permute-start | bytes 3145736 | tf_op jit(solution)/shard_map/while/body/eval_jaxpr/ppermute | solution.py:47
  245.8 7.3 %copy-start = (bf16[2048,2048]{1,0:T(8,128)(2,1)S(1)}, bf16[2048,2048]{1,0:T(8,128)(2,1)}, u32[]{:S(2)}) copy-start(bf16[2048,2048]{1,0:T(8,128)(2,1)} %get-tuple-element.190) | copy-start | bytes 25165828 | tf_op jit(solution)/shard_map/while
  256.9 9.9 %collective-permute-start.4 = (bf16[2048,128]{1,0:T(8,128)(2,1)}, bf16[2048,128]{1,0:T(8,128)(2,1)S(1)}, u32[]{:S(2)}, u32[]{:S(2)}) collective-permute-start(bf16[2048,128]{1,0:T(8,128)(2,1)} %get-tuple-element.55), channel_id=1, source_target_pairs={{0,1},{1,2},{2,3},{3,4},{4,5},{5,6},{6,7},{7,8},{8,9},{9,10},{10,1... | collective-permute-start | bytes 1572872 | tf_op jit(solution)/shard_map/ppermute | solution.py:55
  256.9 9.9 %collective-permute-start.3 = (f32[2048]{0:T(1024)S(1)}, f32[2048]{0:T(1024)S(1)}, u32[]{:S(2)}, u32[]{:S(2)}) collective-permute-start(f32[2048]{0:T(1024)S(1)} %get-tuple-element.54), channel_id=1, source_target_pairs={{0,1},{1,2},{2,3},{3,4},{4,5},{5,6},{6,7},{7,8},{8,9},{9,10},{10,1... | collective-permute-start | bytes 24584 | tf_op jit(solution)/shard_map/ppermute | solution.py:56
  256.9 54.4 %collective-permute-start.5 = (f32[2048,128]{1,0:T(8,128)}, f32[2048,128]{1,0:T(8,128)}, u32[]{:S(2)}, u32[]{:S(2)}) collective-permute-start(f32[2048,128]{1,0:T(8,128)} %get-tuple-element.56), channel_id=1, source_target_pairs={{0,1},{1,2},{2,3},{3,4},{4,5},{5,6},{6,7},{7,8},{8,9},{9,10},{10,1... | collective-permute-start | bytes 3145736 | tf_op jit(solution)/shard_map/ppermute | solution.py:57
  315.0 34.2 %collective-permute-start.6 = (f32[2048,128]{1,0:T(8,128)}, f32[2048,128]{1,0:T(8,128)}, u32[]{:S(2)}, u32[]{:S(2)}) collective-permute-start(f32[2048,128]{1,0:T(8,128)} %get-tuple-element.117), channel_id=1, source_target_pairs={{0,8},{1,9},{2,10},{3,11},{4,12},{5,13},{6,14},{7,15},{8,0},{9,1},... | collective-permute-start | bytes 3145736 | tf_op jit(solution)/shard_map/ppermute | solution.py:74
where the time goes:
time: 353 us; the launch traced here: 352 us
  matrix products  176 us (50%)
  waiting for transfers between devices  104 us (29%)
  blocking collectives  31.5 us (9%)
  other arithmetic  21.5 us (6%)
  local copies, waits for them, and re-layouts  8.6 us (2%)
  loops' own time  4.52 us (1%)
  starting transfers between devices  4.51 us (1%)
    dot_general x9, matrix products, pair_weight(): lax.dot_general(host_x, vis_x, (((1,), (1,)), ((), ())), preferred_elemen...  93.8 us
    ppermute x7, waiting for transfers between devices, full_step(): vis_q = lax.ppermute(vis_q, 'row', forward)  56.2 us
    dot_general x8, matrix products, pair_forces(): jnp.dot(weight_bf, vis_x, preferred_element_type=jnp.float32)  46.1 us
    ppermute x1, waiting for transfers between devices, device_body(): vis_acc = lax.ppermute(vis_acc, 'row', forward)  37.5 us
    psum x1, blocking collectives, device_body(): energy = lax.psum(energy_acc, 'row')  31.5 us
    dot_general x8, matrix products, pair_forces(): lax.dot_general(weight_bf, host_x, (((0,), (0,)), ((), ())), preferred_el...  29.7 us
    while x7, other arithmetic  14.6 us
    ppermute x1, waiting for transfers between devices, device_body(): vis_q = lax.ppermute(vis_q, 'row', forward)  9.87 us
  transfers between devices with their start and end apart: 25, of which 9 were waited for; matrix products, arithmetic and copies ran while one was open for 43% of the time, Pallas kernels for 0%

commit v1 on v0

v1 whole, which is shorter than its diff:
```python
import math

import jax
import jax.numpy as jnp
from jax import lax
from jax.experimental import pallas as pl
from jax.experimental.pallas import tpu as pltpu
from jax.sharding import PartitionSpec as P

MESH = pl.DeviceIdType.MESH
TILE = 256
WIDE = 512
LANE = 128
GROUP = 16
LOG2E = math.log2(math.e)
F32 = jnp.float32
BF16 = jnp.bfloat16


def split3(val):
    high = val.astype(BF16).astype(F32)
    mid = (val - high).astype(BF16).astype(F32)
    return high, mid, val - high - mid


def kernel(n_row, x_hbm, q_ref, force_ref, energy_ref, left_op, pay, xit, aug, xt, qbc, pull, rsum, lim, sgn, sel, part, wbuf, ahead,
           load_sem, ring_send, ring_recv, pair_send, pair_recv, pay_send, pay_recv, ppair_send, ppair_recv, en_send, en_recv):
    n_blk, rows, _ = left_op.shape
    feat = x_hbm.shape[1]
    n_tile = rows // TILE
    n_wide = rows // WIDE
    n_chip = n_row // 2
    chunk = rows // 4
    scale = LOG2E / feat
    me = lax.axis_index("row")
    core = lax.rem(me, 2)
    chip = me // 2
    right = lax.rem(chip + 1, n_chip) * 2 + core
    left = lax.rem(chip + n_chip - 1, n_chip) * 2 + core
    pair = chip * 2 + (1 - core)
    x_lanes = pl.ds(0, feat)
    side_lanes = pl.ds(feat, LANE)

    load = pltpu.make_async_copy(x_hbm, left_op.at[0, :, x_lanes], load_sem)
    load.start()
    barrier = pltpu.get_barrier_semaphore()
    for k in range(1, n_row):
        pl.semaphore_signal(barrier, inc=1, device_id={"row": lax.rem(me + k, n_row)}, device_id_type=MESH)

    def remote(src, dst, send, recv, dev):
        return pltpu.make_async_remote_copy(src_ref=src, dst_ref=dst, send_sem=send, recv_sem=recv, device_id={"row": dev}, device_id_type=MESH)

    def part_of(u, pos):
        return left_op.at[u, pl.ds(pos * chunk, chunk), x_lanes]

    def ring(u, src_pos, to, pos):
        return remote(part_of(u, src_pos), part_of(to, pos), ring_send.at[to, pos], ring_recv.at[to, pos], right if pos == 0 else left)

    def to_pair(u):
        return remote(left_op.at[u, pl.ds(0, 2 * chunk), x_lanes], left_op.at[u, pl.ds(2 * chunk, 2 * chunk), x_lanes],
                      pair_send.at[u], pair_recv.at[u], pair)

    def pay_ring(src, step, pos):
        dst = 2 + step * 4 + pos
        return remote(pay.at[src], pay.at[dst], pay_send.at[step, pos], pay_recv.at[step, pos], right if pos == 0 else left)

    def pay_pair(step):
        at = 2 + step * 4
        return remote(pay.at[pl.ds(at, 2)], pay.at[pl.ds(at + 2, 2)], ppair_send.at[step + 1], ppair_recv.at[step + 1], pair)

    own_pair = remote(left_op.at[0, :, x_lanes], left_op.at[1, :, x_lanes], pair_send.at[1], pair_recv.at[1], pair)
    own_pay_pair = remote(pay.at[0], pay.at[1], ppair_send.at[0], ppair_recv.at[0], pair)

    load.wait()
    pl.semaphore_wait(barrier, n_row - 1)
    for pos in (0, 1):
        ring(0, 0, 2, pos).start()
    own_pair.start()

    lane = lax.broadcasted_iota(jnp.int32, (TILE, LANE), 1)
    table = jnp.zeros((TILE, LANE), F32)
    for g in range(n_tile):
        x32 = left_op[0, pl.ds(g * TILE, TILE), x_lanes].astype(F32)
        half = -0.5 * jnp.sum(x32 * x32, axis=1, keepdims=True)
        q_col = jnp.broadcast_to(q_ref[pl.ds(g, 1), :], (LANE, TILE)).T
        qbc[0, pl.ds(g * TILE, TILE), :] = q_col
        s_parts = split3(jnp.broadcast_to(half, (TILE, LANE)))
        q_parts = split3(q_col)
        base = g * GROUP
        for c, val in enumerate(s_parts + (jnp.ones((TILE, LANE), F32),)):
            hit = (lane >= base + c) & (lane < base + 6) if c == 3 else lane == base + c
            table = jnp.where(hit, val, table)
        for c, val in enumerate(q_parts):
            table = jnp.where(lane == base + 6 + c, val, table)
    pay[0] = table.astype(BF16)

    row_sel = lax.broadcasted_iota(jnp.int32, (LANE, TILE), 0)
    col_sel = lax.broadcasted_iota(jnp.int32, (LANE, TILE), 1) // LANE
    for k in range(n_tile // 2):
        at = row_sel - ((2 * k + col_sel) * GROUP + 6)
        sel[k] = jnp.where((at >= 0) & (at < 3), 1.0, 0.0).astype(BF16)

    own_pay_pair.start()
    for pos in (0, 1):
        pay_ring(0, 0, pos).start()
        for c in range(1, 4):
            ring(0, c, 2 + c, pos).start()

    def transposed(u, g):
        return left_op[u, pl.ds(g * TILE, TILE), x_lanes].T

    sub = lax.broadcasted_iota(jnp.int32, (GROUP, TILE), 0)
    for g in range(n_tile):
        t, cols = g * TILE // WIDE, pl.ds(g * TILE % WIDE, TILE)
        x_t = transposed(0, g)
        xit[t, :, cols] = x_t
        xt[0, :, pl.ds(g * TILE, TILE)] = x_t
        xt[1, :, pl.ds(g * TILE, TILE)] = jnp.zeros_like(x_t)
        left_op[0, pl.ds(g * TILE, TILE), side_lanes] = pay[0]
        x32 = x_t.astype(F32)
        q_row = q_ref[pl.ds(g, 1), :]
        q_log = feat * jnp.maximum(jnp.log(jnp.abs(q_row)), -200.0)
        lim[t, :, cols] = jnp.broadcast_to(q_log, (8, TILE))
        sgn[t, :, cols] = jnp.broadcast_to(jnp.where(q_row < 0.0, -1.0, 1.0), (8, TILE))
        shift = q_log - 0.5 * jnp.sum(x32 * x32, axis=0, keepdims=True)
        strip = jnp.where(sub < 3, 1.0, 0.0)
        for c, val in enumerate(split3(shift)):
            strip = jnp.where(sub == 3 + c, val, strip)
        strip = strip.astype(BF16)
        for k in range(n_tile):
            aug[k, t, :, cols] = jnp.zeros((LANE, TILE), BF16)
            aug[k, t, pl.ds(k * GROUP, GROUP), cols] = strip
    for t in range(n_wide):
        pull[t] = jnp.zeros((feat, WIDE), F32)
        rsum[t] = jnp.zeros((8, WIDE), F32)
    wbuf[...] = jnp.zeros_like(wbuf)

    def quarter_at(u, pos):
        return jnp.where(u < 2, pos, jnp.where(u >= n_blk - 2, u - (n_blk - 2) + 2 * (pos % 2), lax.rem(u + 2, 4)))

    def table_at(u, pos):
        return jnp.where(u < 2, u, ((u + 2) // 4) * 4 + pos - 2)

    def cross(u, t, g):
        rhs = jnp.concatenate([xit[t], aug[2 * quarter_at(u, g // 2) + g % 2, t]], axis=0)
        return jnp.dot(left_op[u, pl.ds(g * TILE, TILE), :], rhs, preferred_element_type=F32)

    def pulled(slot, t, g):
        at = pl.ds(g * TILE, TILE)
        pull[t] += jnp.dot(xt[slot, :, at], wbuf[at, :], preferred_element_type=F32)

    def prepare(u, slot, pos):
        strip = pay[table_at(u, pos)]
        wide = jnp.dot(strip, sel[quarter_at(u, pos)], preferred_element_type=F32)
        for h in (0, 1):
            at = pl.ds((2 * pos + h) * TILE, TILE)
            left_op[u, at, side_lanes] = strip
            qbc[slot, at, :] = wide[:, h * LANE:(h + 1) * LANE]
            xt[slot, :, at] = transposed(u, 2 * pos + h)

    def columns(u, t, own, todo):
        now = lax.rem(u, 2)
        nxt = jnp.minimum(u + 1, n_blk - 1)
        t_next = lax.rem(t + 1, n_wide)
        u_next = jnp.where(t == n_wide - 1, nxt, u)
        t_prev = lax.rem(t + n_wide - 1, n_wide)
        slot_prev = jnp.where(t == 0, 1 - now, now)
        bound = lim[t][None]
        sums = jnp.zeros((8, WIDE), F32)
        dots = ahead[...]
        for g in range(n_tile):
            pulled(slot_prev, t_prev, g)
            if g + 1 < n_tile:
                later = cross(u, t, g + 1)
            else:
                ahead[...] = cross(u_next, t_next, 0)
            if g % (n_tile // max(1, len(todo))) == 0 and todo:
                prepare(nxt, 1 - now, todo[g // (n_tile // len(todo))])
            at = pl.ds(g * TILE, TILE)
            q_col = qbc[now, at, :]
            kern = jnp.exp2(jnp.minimum(dots.reshape(TILE // 8, 8, WIDE), bound) * scale).reshape(TILE, WIDE)
            w = kern * jnp.concatenate([q_col] * (WIDE // LANE), axis=1)
            if own:
                r_id = lax.broadcasted_iota(jnp.int32, (TILE, WIDE), 0) + g * TILE
                c_id = lax.broadcasted_iota(jnp.int32, (TILE, WIDE), 1) + t * WIDE
                w = jnp.where(r_id == c_id, 0.0, w)
            sums = sums + jnp.sum(w.reshape(TILE // 8, 8, WIDE), axis=0)
            wbuf[at, :] = w.astype(BF16)
            if g + 1 < n_tile:
                dots = later
        rsum[t] += sums

    def pass_on(u):
        for pos in (0, 1):
            ring(u, pos, u, pos).wait_recv()
        to_pair(u).start()

        @pl.when(u < n_blk - 4)
        def _():
            ring(u, 0, u + 4, 0).start()

        @pl.when(u < n_blk - 6)
        def _():
            ring(u, 1, u + 4, 1).start()

        @pl.when((u >= n_blk - 4) & (u < n_blk - 2))
        def _():
            ring(u, 1, u + 2, 1).start()

        @pl.when(lax.rem(u, 4) == 2)
        def _():
            step = (u - 2) // 4
            for pos in (0, 1):
                pay_ring(2 + step * 4 + pos, step, pos).wait_recv()
            pay_pair(step).start()

            @pl.when(step < 3)
            def _():
                for pos in (0, 1):
                    pay_ring(2 + step * 4 + pos, step + 1, pos).start()

    half = n_wide // 2

    def loop(first, last, fn):
        def step(t, carry):
            fn(t)
            return carry

        lax.fori_loop(first, last, step, 0)

    chunks = [tuple(range(4))[k * 4 // half:(k + 1) * 4 // half] for k in range(half)]
    ahead[...] = cross(0, 0, 0)
    loop(0, half, lambda t: columns(0, t, True, ()))
    own_pair.wait_recv()
    own_pay_pair.wait_recv()
    for k in range(half):
        columns(0, half + k, True, chunks[k])

    def other(u):
        @pl.when(u < n_blk - 1)
        def _():
            pass_on(u + 1)

        loop(0, half, lambda t: columns(u, t, False, ()))

        @pl.when(u < n_blk - 1)
        def _():
            to_pair(u + 1).wait_recv()

            @pl.when(lax.rem(u + 1, 4) == 2)
            def _():
                pay_pair((u - 1) // 4).wait_recv()

        for k in range(half):
            columns(u, half + k, False, chunks[k])

    loop(1, n_blk, other)
    for g in range(n_tile):
        pulled((n_blk - 1) % 2, n_wide - 1, g)

    total = jnp.zeros((8, WIDE), F32)
    for t in range(n_wide):
        total = total + rsum[t] * sgn[t]
    part[me] = sum(total[:, k * LANE:(k + 1) * LANE] for k in range(WIDE // LANE))

    def finish(t):
        sums = jnp.sum(rsum[t], axis=0, keepdims=True)
        force_t = (sums * xit[t].astype(F32) - pull[t]) * (sgn[t, pl.ds(0, 1), :] * (1.0 / feat))
        force_ref[pl.ds(pl.multiple_of(t * WIDE, WIDE), WIDE), :] = force_t.T

    finish(0)

    def en_copy(k):
        return remote(part.at[me], part.at[me], en_send.at[k - 1], en_recv.at[k - 1], lax.rem(me + k, n_row))

    for k in range(1, n_row):
        en_copy(k).start()
    loop(1, n_wide, finish)

    for pos in (0, 1):
        for to in range(2, n_blk):
            ring(0, 0, to, pos).wait_send()
        for step in range(4):
            pay_ring(0, step, pos).wait_send()
    own_pair.wait_send()
    own_pay_pair.wait_send()
    for u in range(2, n_blk):
        to_pair(u).wait_send()
    for step in range(4):
        pay_pair(step).wait_send()
    for k in range(1, n_row):
        source = lax.rem(me + n_row - k, n_row)
        remote(part.at[source], part.at[source], en_send.at[k - 1], en_recv.at[k - 1], me).wait_recv()
        en_copy(k).wait_send()
    energy = part[0]
    for r in range(1, n_row):
        energy = energy + part[r]
    energy_ref[...] = jnp.broadcast_to(0.5 * jnp.sum(jnp.sum(energy, axis=0, keepdims=True), axis=1, keepdims=True), (8, LANE))


def solution(mesh):
    n_row = mesh.shape["row"]

    def device_body(pos_loc, chg_loc):
        rows, feat = pos_loc.shape
        n_tile, n_wide = rows // TILE, rows // WIDE
        vmem = pl.BlockSpec(memory_space=pltpu.VMEM)
        dma = pltpu.SemaphoreType.DMA
        force, energy = pl.pallas_call(
            lambda *refs: kernel(n_row, *refs),
            out_shape=(jax.ShapeDtypeStruct((rows, feat), F32), jax.ShapeDtypeStruct((8, LANE), F32)),
            in_specs=[pl.BlockSpec(memory_space=pl.ANY), vmem],
            out_specs=(vmem, vmem),
            scratch_shapes=[
                pltpu.VMEM((n_row, rows, feat + LANE), BF16),
                pltpu.VMEM((n_row + 2, TILE, LANE), BF16),
                pltpu.VMEM((n_wide, feat, WIDE), BF16),
                pltpu.VMEM((n_tile, n_wide, LANE, WIDE), BF16),
                pltpu.VMEM((2, feat, rows), BF16),
                pltpu.VMEM((2, rows, LANE), F32),
                pltpu.VMEM((n_wide, feat, WIDE), F32),
                pltpu.VMEM((n_wide, 8, WIDE), F32),
                pltpu.VMEM((n_wide, 8, WIDE), F32),
                pltpu.VMEM((n_wide, 8, WIDE), F32),
                pltpu.VMEM((n_tile // 2, LANE, TILE), BF16),
                pltpu.VMEM((n_row, 8, LANE), F32),
                pltpu.VMEM((rows, WIDE), BF16),
                pltpu.VMEM((TILE, WIDE), F32),
                dma,
                dma((n_row, 2)),
                dma((n_row, 2)),
                dma((n_row,)),
                dma((n_row,)),
                dma((4, 2)),
                dma((4, 2)),
                dma((5,)),
                dma((5,)),
                dma((n_row - 1,)),
                dma((n_row - 1,)),
            ],
            compiler_params=pltpu.CompilerParams(collective_id=0, has_side_effects=True, vmem_limit_bytes=60 * 2**20),
        )(pos_loc, chg_loc.reshape(n_tile, TILE))
        return force, energy[0, :1]

    return jax.shard_map(device_body, mesh=mesh, in_specs=(P(("sys", "row"), None), P(("sys", "row"))), out_specs=(P(("sys", "row"), None), P("sys")), check_vma=False)
```

time: 353 us -> 105 us (0.30)
  matrix products: 176 us -> 0 us
  waiting for transfers between devices: 104 us -> 0 us
  Pallas kernels: 0 us -> 98.7 us
  blocking collectives: 31.5 us -> 0 us
  other arithmetic: 21.5 us -> 0 us
  loops' own time: 4.52 us -> 0 us
  starting transfers between devices: 4.51 us -> 0 us
  local copies, waits for them, and re-layouts: 8.6 us -> 4.75 us
    dot_general x26 -> x0, matrix products: 176 us -> none  [the longest x9 93.8 us: pair_weight(): lax.dot_general(host_x, vis_x, (((1,), (1,)), ((), ())), preferred_elemen...]
    ppermute x25 -> x0, waiting for transfers between devices: 104 us -> none  [the longest x7 56.2 us: full_step(): vis_q = lax.ppermute(vis_q, 'row', forward)]
    pallas_call x0 -> x1, Pallas kernels: none -> 98.7 us  [device_body(): pl.pallas_call(lambda *refs: kernel(n_row, *refs), out_shape=(jax.ShapeDt...]
    psum x1 -> x0, blocking collectives: 31.5 us -> none  [device_body(): energy = lax.psum(energy_acc, 'row')]
    while x7 -> x0, other arithmetic: 14.6 us -> none
    while x28 -> x0, local copies, waits for them, and re-layouts: 5.97 us -> none
    another operation x1 -> x0, loops' own time: 4.52 us -> none  [device_body(): lax.fori_loop(0, full_steps, full_step, loop_state)]
    ppermute x25 -> x0, starting transfers between devices: 4.51 us -> none  [the longest x7 2.23 us: full_step(): vis_q = lax.ppermute(vis_q, 'row', forward)]
  transfers between devices with their start and end apart: 25 -> 0, of which waited for: 9 -> 0; matrix products, arithmetic and copies ran while one was open for 43% -> 0% of each run, Pallas kernels for 0% -> 0%
where the time goes in v1:
time: 105 us; the launch traced here: 104 us
  Pallas kernels  98.7 us (94%)
  local copies, waits for them, and re-layouts  4.75 us (5%)
    pallas_call x1, Pallas kernels, device_body(): pl.pallas_call(lambda *refs: kernel(n_row, *refs), out_shape=(jax.ShapeDt...  98.7 us
    unnamed x1, local copies, waits for them, and re-layouts  2.26 us

profile of v1, /device:TPU:30, one launch (start us, length us, event | category | flops | bytes accessed | tf_op | source)
XLA Modules:
  0.0 104.1 jit_solution(16444433325556604962)
XLA Ops:
  0.6 1.3 %reshape.7.refs_1_ = f32[8,256]{1,0:T(8,128)} reshape(f32[2048]{0:T(1024)} %param.3) | data formatting | bytes 16384 | tf_op jit(solution)/shard_map/reshape | solution.py:342
  1.9 98.7 %shard_map.41 = (f32[2048,128]{1,0:T(8,128)}, f32[8,128]{1,0:T(8,128)}) custom-call(bf16[2048,128]{1,0:T(8,128)(2,1)} %refs_0_.1, f32[8,256]{1,0:T(8,128)} %reshape.7.refs_1_), custom_call_target="tpu_custom_call" | custom-call | tf_op jit(solution)/shard_map/pallas_call | solution.py:309
  100.6 1.2 %slice.3 = f32[1,1]{1,0:T(1,128)} slice(f32[8,128]{1,0:T(8,128)} %get-tuple-element.5), slice={[0:1], [0:1]} | slice | bytes 8 | tf_op jit(solution)/shard_map/slice | solution.py:343
  101.8 2.3 %copy.5 = f32[2048,128]{1,0:T(8,128)} copy(f32[2048,128]{1,0:T(8,128)} %get-tuple-element.8) | data formatting | bytes 2097152
